TPU v7x, 32 devices: a whole 2x2x4 slice. The times are simulated.
32 devices in a mesh: dp: 2 (over core), tensor: 16 (over z, y, x).
Axes of the slice: x: 2, y: 2, z: 4, core: 2. Of those that a mesh axis runs over, the one named last changes fastest.
Arguments:
- resid_stream: bfloat16 [512, 4608], P(('dp', 'tensor')), parts along dimension 0, may hold values from -120 to 120, as said below
- pre_gain: float32 [4608], replicated, may hold values from 0.5 to 1.5
- w_gate: bfloat16 [4608, 6144], P(None, 'tensor'), may hold values from -0.09375 to 0.09375
- w_up: bfloat16 [4608, 6144], P(None, 'tensor'), may hold values from -0.09375 to 0.09375
- w_down: bfloat16 [6144, 4608], P('tensor'), may hold values from -0.078125 to 0.078125
- post_gain: float32 [4608], replicated, may hold values from 0.5 to 1.5
Outputs:
- resid_out: bfloat16 [512, 4608], P(('dp', 'tensor')), parts along dimension 0
There are 2 independent parts, one for each index of `dp`. A program takes and returns all parts, laid end to end along the dimension named above; an argument that names none is the same for every part. Nothing has to cross between parts.
Inputs may be any that keep to these rules, and one draw needn't show every extreme that they name: `resid_stream`: entries are real-valued.
All inputs are finite; a program needn't handle non-finite values.
Results may differ from a plain program's by a relative error of at most 0.0029.
Values may be sent and summed in bfloat16 or wider, within the bound.
A program may use at most 128 MiB of HBM per device.

v0:
```python
import functools

import jax
import jax.numpy as jnp
from jax import lax
from jax.experimental import pallas as pl
from jax.experimental.pallas import tpu as pltpu
from jax.sharding import PartitionSpec as P

norm_eps = 1e-06
SIDE = 2
PLANE = SIDE * SIDE
TURNED = 4
LINE = 4
MESH = pl.DeviceIdType.MESH


def shards(resid_stream, pre_gain, w_gate, w_up, w_down, post_gain):
    stream = resid_stream.astype(jnp.float32)
    local_norm = stream * lax.rsqrt(jnp.mean(stream * stream, axis=1, keepdims=True) + norm_eps)
    normed = (local_norm * pre_gain).astype(jnp.bfloat16)
    row_piece = lax.all_gather(normed, "tensor", axis=0, tiled=True)
    gate_out = jnp.dot(row_piece, w_gate, preferred_element_type=jnp.float32)
    up_out = jnp.dot(row_piece, w_up, preferred_element_type=jnp.float32)
    hidden = (jax.nn.gelu(gate_out, approximate=True) * up_out).astype(jnp.bfloat16)
    block_rows = lax.psum_scatter(
        jnp.dot(hidden, w_down, preferred_element_type=jnp.float32),
        "tensor",
        scatter_dimension=0,
        tiled=True,
    )
    row_factor = lax.rsqrt(jnp.mean(block_rows * block_rows, axis=1, keepdims=True) + norm_eps)
    post = (block_rows * row_factor * post_gain).astype(jnp.bfloat16)
    post = lax.optimization_barrier(post)
    return (stream + post.astype(jnp.float32)).astype(jnp.bfloat16)


def tile_of(size, most):
    return max(t for t in range(128, most + 1, 128) if size % t == 0)


def cut(d):
    lanes = d // 128
    most = 2 * (TURNED * lanes // 36) + lanes % 2
    return (lanes - most) // 2 * 128, most * 128


def kernel(
    stream_ref, pre_ref, wg_hbm, wu_hbm, wd_hbm, post_ref, out_ref,
    w1, w2, gath, gu, hid, part, sendb, rda, rdb, xr, yr, zr,
    zrc, xyc,
    wsem, ssem, agz, agx, agy, agd, rsd, rsx, rsy, rsz, agp, agc, rsc, rsp,
):
    rows, d = stream_ref.shape
    ff = wg_hbm.shape[1]
    half, cw = cut(d)
    group = PLANE * rows
    A, B = halves = pl.ds(0, half), pl.ds(half, half)
    C = pl.ds(2 * half, cw)

    me = lax.axis_index("tensor")
    x = lax.rem(me, SIDE)
    y = lax.rem(lax.div(me, SIDE), SIDE)
    z = lax.div(me, PLANE)
    spot = lax.rem(me, PLANE)
    sx = 1 - 2 * x
    sy = SIDE * (1 - 2 * y)
    xn, yn, dn = me + sx, me + sy, me + sx + sy
    flip = lax.div(z, LINE // 2)
    p = z + flip * (LINE - 1 - 2 * z)
    inner, outer = p == 1, p == 0
    far = me + PLANE * (1 - 2 * flip)
    near = me - PLANE * (1 - 2 * flip)

    barrier = pltpu.get_barrier_semaphore()
    for other in (xn, yn, dn, far):
        pl.semaphore_signal(barrier, inc=1, device_id={"tensor": other}, device_id_type=MESH)

    @pl.when(inner)
    def _():
        pl.semaphore_signal(barrier, inc=1, device_id={"tensor": near}, device_id_type=MESH)

    loads = [
        pltpu.make_async_copy(wg_hbm, w1.at[:, pl.ds(0, ff)], wsem.at[0]),
        pltpu.make_async_copy(wu_hbm, w1.at[:, pl.ds(ff, ff)], wsem.at[1]),
        pltpu.make_async_copy(wd_hbm, w2, wsem.at[2]),
    ]
    for load in loads:
        load.start()

    def plane_of(v):
        return v + flip * (LINE - 1 - 2 * v)

    order = [plane_of(p), plane_of(1 - p), plane_of(2), plane_of(3)]

    def blk(s, shift):
        return pl.ds(pl.multiple_of((s * PLANE + spot + shift) * rows, rows), rows)

    pending = []

    def send(src, dst, recv_sem, target, cond=None, inside=False):
        copy = pltpu.make_async_remote_copy(
            src_ref=src, dst_ref=dst, send_sem=ssem.at[len(pending)], recv_sem=recv_sem,
            device_id={"tensor": target}, device_id_type=MESH,
        )
        pending.append((cond, src.shape))
        if cond is None or inside:
            copy.start()
        else:
            pl.when(cond)(copy.start)

    def arrive(dst, recv_sem):
        pltpu.make_async_remote_copy(
            src_ref=dst, dst_ref=dst, send_sem=ssem.at[0], recv_sem=recv_sem,
            device_id={"tensor": xn}, device_id_type=MESH,
        ).wait_recv()

    stream = stream_ref[...].astype(jnp.float32)
    scale = lax.rsqrt(jnp.mean(stream * stream, axis=1, keepdims=True) + norm_eps)
    gath[blk(z, 0), :] = (stream * scale * pre_ref[...][None]).astype(jnp.bfloat16)

    pl.semaphore_wait(barrier, 4 + p)

    def along(k, kind):
        s = order[k]
        ref = gath.at[blk(s, 0), halves[kind]]
        if k > 0:
            arrive(ref, agz.at[kind, s])
        if k == 0:
            send(ref, ref, agz.at[kind, s], far)
        if k == 1:
            send(ref, ref, agz.at[kind, s], far, inner)
        else:
            send(ref, ref, agz.at[kind, s], near, inner)
        send(ref, ref, agx.at[kind, s], xn)
        if kind == 1:
            send(ref, ref, agy.at[kind, s], yn)
            ref = gath.at[blk(s, 0), A]
            send(ref, ref, agy.at[0, s], yn)

    def across(k):
        s = order[k]
        ref = gath.at[blk(s, sx), A]
        arrive(ref, agx.at[0, s])
        send(ref, ref, agd.at[0, s], yn)
        ref = gath.at[blk(s, sy), B]
        arrive(ref, agy.at[1, s])
        send(ref, ref, agd.at[1, s], xn)

    around = ((sx, xn), (sy, yn), (sx + sy, dn))

    def plane(s):
        return pl.ds(pl.multiple_of(s * group, group), group)

    def spread():
        ref = gath.at[blk(z, 0), C]
        for i, (_, other) in enumerate(around):
            send(ref, ref, agp.at[i], other)

    def relay(k):
        s = order[k]
        ref = gath.at[plane(s), C]
        if k == 0:
            for i, (shift, _) in enumerate(around):
                arrive(gath.at[blk(s, shift), C], agp.at[i])
            send(ref, ref, agc.at[s], far)
        else:
            arrive(ref, agc.at[s])
        if k == 1:
            send(ref, ref, agc.at[s], far, inner)
        else:
            send(ref, ref, agc.at[s], near, inner)

    tile = tile_of(2 * ff, 256)

    def first_dots(k):
        s = order[k]
        arrive(gath.at[blk(s, sx), B], agx.at[1, s])
        arrive(gath.at[blk(s, sy), A], agy.at[0, s])
        arrive(gath.at[blk(s, sx + sy), A], agd.at[0, s])
        arrive(gath.at[blk(s, sx + sy), B], agd.at[1, s])
        if k == 0:
            loads[0].wait()
            loads[1].wait()
        at = pl.ds(pl.multiple_of(s * group, group), group)

        @pl.loop(0, 2 * ff // tile)
        def _(i):
            cols = pl.ds(pl.multiple_of(i * tile, tile), tile)
            gu[:, cols] = jnp.dot(gath[at, :], w1[:, cols], preferred_element_type=jnp.float32)

        gate, up = gu[:, :ff], gu[:, ff:]
        hid[at, :] = (jax.nn.gelu(gate, approximate=True) * up).astype(jnp.bfloat16)

    spread()
    along(0, 0)
    along(0, 1)
    along(1, 0)
    across(0)
    along(1, 1)
    relay(0)
    along(2, 0)
    across(1)
    along(2, 1)
    first_dots(0)
    along(3, 0)
    across(2)
    along(3, 1)
    relay(1)
    relay(2)
    across(3)
    first_dots(1)
    relay(3)
    first_dots(2)
    first_dots(3)

    back = order[::-1]
    wide = tile_of(d, 768)

    def last_dot(j):
        s = back[j]
        if j == 0:
            loads[2].wait()
        at = pl.ds(pl.multiple_of(s * group, group), group)

        @pl.loop(0, d // wide)
        def _(i):
            cols = pl.ds(pl.multiple_of(i * wide, wide), wide)
            res = jnp.dot(hid[at, :], w2[:, cols], preferred_element_type=jnp.float32)
            part[at, cols] = res
            sendb[at, cols] = res.astype(jnp.bfloat16)

        send(sendb.at[blk(s, sx + sy), A], rda.at[s], rsd.at[0, s], xn)
        send(sendb.at[blk(s, sx + sy), B], rdb.at[s], rsd.at[1, s], yn)
        send(sendb.at[blk(s, sx), A], xr.at[s, :, A], rsx.at[0, s], xn)
        send(sendb.at[blk(s, sy), B], yr.at[s, :, B], rsy.at[1, s], yn)

    def pass_on(j):
        s = back[j]
        arrive(rda.at[s], rsd.at[0, s])
        at = blk(s, sy)
        sendb[at, A] = (part[at, A] + rda[s].astype(jnp.float32)).astype(jnp.bfloat16)
        send(sendb.at[at, A], yr.at[s, :, A], rsy.at[0, s], yn)
        arrive(rdb.at[s], rsd.at[1, s])
        at = blk(s, sx)
        sendb[at, B] = (part[at, B] + rdb[s].astype(jnp.float32)).astype(jnp.bfloat16)
        send(sendb.at[at, B], xr.at[s, :, B], rsx.at[1, s], xn)

    def settle(j):
        s = back[j]
        arrive(xr.at[s, :, A], rsx.at[0, s])
        arrive(yr.at[s, :, B], rsy.at[1, s])
        at = blk(s, 0)
        for kind, cols in enumerate(halves):
            if kind == 0:
                arrive(yr.at[s, :, A], rsy.at[0, s])
            else:
                arrive(xr.at[s, :, B], rsx.at[1, s])
            total = part[at, cols] + xr[s, :, cols].astype(jnp.float32) + yr[s, :, cols].astype(jnp.float32)
            part[at, cols] = total
            if j < LINE - 1:
                pl.when(outer)(functools.partial(ship, j, kind, far, flip, outer))

    def ship(j, kind, target, way, cond):
        s = back[j]
        at = blk(s, 0)
        sendb[at, halves[kind]] = part[at, halves[kind]].astype(jnp.bfloat16)
        send(sendb.at[at, halves[kind]], zr.at[way, s, :, halves[kind]], rsz.at[way, kind, s], target, cond, True)

    def add(j, way, kind):
        s = back[j]
        at = blk(s, 0)
        arrive(zr.at[way, s, :, halves[kind]], rsz.at[way, kind, s])
        part[at, halves[kind]] += zr[way, s, :, halves[kind]].astype(jnp.float32)

    outward, inward = flip, 1 - flip

    def follow(j):
        @pl.when(inner)
        def _():
            for kind in (0, 1):
                if j == LINE - 2:
                    add(j, inward, kind)
                    ship(j, kind, near, inward, inner)
                else:
                    add(j, outward, kind)
                    ship(j, kind, far, outward, inner)

    def turn(j):
        s = back[j]
        send(sendb.at[plane(s), C], zrc.at[flip, s], rsc.at[flip, s], far, outer)

    def add_turned(s, way):
        arrive(zrc.at[way, s], rsc.at[way, s])
        part[plane(s), C] += zrc[way, s].astype(jnp.float32)

    def turn_on(j):
        @pl.when(inner)
        def _():
            s = back[j]
            way, target = (inward, near) if j == LINE - 2 else (outward, far)
            add_turned(s, way)
            sendb[plane(s), C] = part[plane(s), C].astype(jnp.bfloat16)
            send(sendb.at[plane(s), C], zrc.at[way, s], rsc.at[way, s], target, inner, True)

    def share():
        s = back[LINE - 1]
        add_turned(s, inward)
        pl.when(inner)(lambda: add_turned(back[LINE - 1], outward))
        sendb[plane(s), C] = part[plane(s), C].astype(jnp.bfloat16)
        for i, (shift, other) in enumerate(around):
            send(sendb.at[blk(s, shift), C], xyc.at[i], rsp.at[i], other)

    def gain():
        for i in range(len(around)):
            arrive(xyc.at[i], rsp.at[i])
        at = blk(z, 0)
        part[at, C] += xyc[0].astype(jnp.float32) + xyc[1].astype(jnp.float32) + xyc[2].astype(jnp.float32)

    def close():
        for kind in (0, 1):
            add(LINE - 1, inward, kind)
            pl.when(inner)(functools.partial(add, LINE - 1, outward, kind))

    last_dot(0)
    turn(0)
    last_dot(1)
    turn(1)
    pass_on(0)
    last_dot(2)
    turn(2)
    pass_on(1)
    turn_on(0)
    last_dot(3)
    settle(0)
    turn_on(1)
    pass_on(2)
    follow(0)
    turn_on(2)
    settle(1)
    pass_on(3)
    follow(1)
    settle(2)
    share()
    follow(2)
    settle(3)
    close()
    gain()

    total = part[blk(z, 0), :]
    factor = lax.rsqrt(jnp.mean(total * total, axis=1, keepdims=True) + norm_eps)
    post = (total * factor * post_ref[...][None]).astype(jnp.bfloat16)
    stream = stream_ref[...].astype(jnp.float32)
    out_ref[...] = (stream + post.astype(jnp.float32)).astype(jnp.bfloat16)

    def drain(i, size):
        sent = sendb.at[pl.ds(0, size[0]), pl.ds(0, size[1])]
        pltpu.make_async_remote_copy(
            src_ref=sent, dst_ref=sent, send_sem=ssem.at[i], recv_sem=rsd.at[0, 0],
            device_id={"tensor": xn}, device_id_type=MESH,
        ).wait_send()

    for i, (cond, size) in enumerate(pending):
        if cond is None:
            drain(i, size)
        else:
            pl.when(cond)(functools.partial(drain, i, size))


def fused(resid_stream, pre_gain, w_gate, w_up, w_down, post_gain):
    rows, d = resid_stream.shape
    ff = w_gate.shape[1]
    half, cw = cut(d)
    n = PLANE * LINE
    bf, f32, dma = jnp.bfloat16, jnp.float32, pltpu.SemaphoreType.DMA
    vmem = pl.BlockSpec(memory_space=pltpu.VMEM)
    hbm = pl.BlockSpec(memory_space=pl.ANY)
    return pl.pallas_call(
        kernel,
        out_shape=jax.ShapeDtypeStruct((rows, d), bf),
        in_specs=[vmem, vmem, hbm, hbm, hbm, vmem],
        out_specs=vmem,
        scratch_shapes=[
            pltpu.VMEM((d, 2 * ff), bf),
            pltpu.VMEM((ff, d), bf),
            pltpu.VMEM((n * rows, d), bf),
            pltpu.VMEM((PLANE * rows, 2 * ff), f32),
            pltpu.VMEM((n * rows, ff), bf),
            pltpu.VMEM((n * rows, d), f32),
            pltpu.VMEM((n * rows, d), bf),
            pltpu.VMEM((LINE, rows, half), bf),
            pltpu.VMEM((LINE, rows, half), bf),
            pltpu.VMEM((LINE, rows, d), bf),
            pltpu.VMEM((LINE, rows, d), bf),
            pltpu.VMEM((2, LINE, rows, d), bf),
            pltpu.VMEM((2, LINE, PLANE * rows, cw), bf),
            pltpu.VMEM((3, rows, cw), bf),
            dma((3,)),
            dma((144,)),
            dma((2, LINE)),
            dma((2, LINE)),
            dma((2, LINE)),
            dma((2, LINE)),
            dma((2, LINE)),
            dma((2, LINE)),
            dma((2, LINE)),
            dma((2, 2, LINE)),
            dma((3,)),
            dma((LINE,)),
            dma((2, LINE)),
            dma((3,)),
        ],
        compiler_params=pltpu.CompilerParams(
            collective_id=0, has_side_effects=True, vmem_limit_bytes=60 * 2**20
        ),
        name="ffn",
    )(resid_stream, pre_gain, w_gate, w_up, w_down, post_gain)


def solution(mesh):
    body = fused if mesh.shape["tensor"] == PLANE * LINE else shards
    return jax.shard_map(
        body,
        mesh=mesh,
        in_specs=(
            P(("dp", "tensor"), None),
            P(),
            P(None, "tensor"),
            P(None, "tensor"),
            P("tensor", None),
            P(),
        ),
        out_specs=P(("dp", "tensor"), None),
        check_vma=False,
    )
```

profile of v0, /device:TPU:0, one launch (start us, length us, event | category | flops | bytes accessed | tf_op | source)
XLA Modules:
  0.0 57.8 jit_solution(6661662231943653531)
XLA Ops:
  0.0 56.2 %ffn.1 = bf16[16,4608]{1,0:T(8,128)(2,1)} custom-call(bf16[16,4608]{1,0:T(8,128)(2,1)} %stream_ref.1, f32[4608]{0:T(1024)} %pre_ref.1, bf16[4608,384]{1,0:T(8,128)(2,1)} %wg_hbm.1, bf16[4608,384]{1,0:T(8,128)(2,1)} %wu_hbm.1, bf16[384,4608]{1,0:T(8,128)(2,1)} %wd_hbm.1, f32[4608]{0:T(1024)} %post_ref.1), custom_call_target="tpu_custom_call" | custom-call | tf_op jit(solution)/shard_map/ffn/pallas_call | solution.py:378
  56.2 1.6 %copy.8 = bf16[16,4608]{1,0:T(8,128)(2,1)} copy(bf16[16,4608]{1,0:T(8,128)(2,1)} %ffn.1) | data formatting | bytes 294912
where the time goes:
time: 58 us; the launch traced here: 57.8 us
  Pallas kernels  56.2 us (97%)
  local copies, waits for them, and re-layouts  1.58 us (3%)
    pallas_call x1, Pallas kernels, fused(): pl.pallas_call(kernel, out_shape=jax.ShapeDtypeStruct((rows, d), bf), in_...  56.2 us
    unnamed x1, local copies, waits for them, and re-layouts  1.58 us

commit v1 on v0

v1 whole, which is shorter than its diff:
```python
import functools

import jax
import jax.numpy as jnp
from jax import lax
from jax.experimental import pallas as pl
from jax.experimental.pallas import tpu as pltpu
from jax.sharding import PartitionSpec as P

norm_eps = 1e-06
SIDE = 2
PLANE = SIDE * SIDE
TURNED = 4
LINE = 4
MESH = pl.DeviceIdType.MESH


def shards(resid_stream, pre_gain, w_gate, w_up, w_down, post_gain):
    stream = resid_stream.astype(jnp.float32)
    local_norm = stream * lax.rsqrt(jnp.mean(stream * stream, axis=1, keepdims=True) + norm_eps)
    normed = (local_norm * pre_gain).astype(jnp.bfloat16)
    row_piece = lax.all_gather(normed, "tensor", axis=0, tiled=True)
    gate_out = jnp.dot(row_piece, w_gate, preferred_element_type=jnp.float32)
    up_out = jnp.dot(row_piece, w_up, preferred_element_type=jnp.float32)
    hidden = (jax.nn.gelu(gate_out, approximate=True) * up_out).astype(jnp.bfloat16)
    block_rows = lax.psum_scatter(
        jnp.dot(hidden, w_down, preferred_element_type=jnp.float32),
        "tensor",
        scatter_dimension=0,
        tiled=True,
    )
    row_factor = lax.rsqrt(jnp.mean(block_rows * block_rows, axis=1, keepdims=True) + norm_eps)
    post = (block_rows * row_factor * post_gain).astype(jnp.bfloat16)
    post = lax.optimization_barrier(post)
    return (stream + post.astype(jnp.float32)).astype(jnp.bfloat16)


def tile_of(size, most):
    return max(t for t in range(128, most + 1, 128) if size % t == 0)


def cut(d):
    lanes = d // 128
    most = 2 * (TURNED * lanes // 36) + lanes % 2
    return (lanes - most) // 2 * 128, most * 128


ARRIVALS = [
    *((name, q) for name in ("xa", "yb", "rest", "da", "db", "ra", "rb") for q in range(LINE)),
    *((name, j) for name in ("za", "zb", "zo", "zc", "sa", "sb", "sc") for j in range(LINE - 1)),
    ("spread", 0),
    ("share", 0),
]
BATCH = 32
SENDS = 8


def kernel(
    stream_hbm, pre_hbm, wg_hbm, wu_hbm, wd_hbm, post_hbm, out_ref,
    stream_ref, pre_ref, post_ref, w1, w2, gath, gu, hid, part, sendb, rda, rdb, rr, zr, zc, xyc,
    lsem, ssem, rsem,
):
    rows, d = stream_ref.shape
    ff = wg_hbm.shape[1]
    half, cw = cut(d)
    group = PLANE * rows
    A, B = halves = pl.ds(0, half), pl.ds(half, half)
    AB = pl.ds(0, 2 * half)
    C = pl.ds(2 * half, cw)

    me = lax.axis_index("tensor")
    x = lax.rem(me, SIDE)
    y = lax.rem(lax.div(me, SIDE), SIDE)
    z = lax.div(me, PLANE)
    sx = 1 - 2 * x
    sy = SIDE * (1 - 2 * y)
    xn, yn, dn = me + sx, me + sy, me + sx + sy
    flip = lax.div(z, LINE // 2)
    step = PLANE * (1 - 2 * flip)
    place = z + flip * (LINE - 1 - 2 * z)
    far, near = me + step, me - step

    barrier = pltpu.get_barrier_semaphore()
    for other in (xn, yn, dn, far):
        pl.semaphore_signal(barrier, inc=1, device_id={"tensor": other}, device_id_type=MESH)

    @pl.when(place == 1)
    def _():
        pl.semaphore_signal(barrier, inc=1, device_id={"tensor": near}, device_id_type=MESH)

    loads = [
        pltpu.make_async_copy(src, dst, lsem.at[i])
        for i, (src, dst) in enumerate(
            (
                (stream_hbm, stream_ref),
                (pre_hbm, pre_ref),
                (wg_hbm, w1.at[:, pl.ds(0, ff)]),
                (wu_hbm, w1.at[:, pl.ds(ff, ff)]),
                (wd_hbm, w2),
                (post_hbm, post_ref),
            )
        )
    ]
    for load in loads:
        load.start()
    loads[0].wait()
    loads[1].wait()

    def blk(q, r, n=1):
        return pl.ds((q * PLANE + r) * rows, n * rows)

    def normed():
        stream = stream_ref[...].astype(jnp.float32)
        scale = lax.rsqrt(jnp.mean(stream * stream, axis=1, keepdims=True) + norm_eps)
        return (stream * scale * pre_ref[...][None]).astype(jnp.bfloat16)

    def run(p):
        sent = []

        def send(src, dst, name, target):
            width = src.shape[-1]
            units = src.size // (rows * width) if hasattr(src, "size") else src.shape[0] // rows
            for slot, entry in enumerate(sent):
                if entry[0] == width and entry[1] + units <= BATCH:
                    entry[1] += units
                    break
            else:
                slot = len(sent)
                sent.append([width, units])
            pltpu.make_async_remote_copy(
                src_ref=src, dst_ref=dst, send_sem=ssem.at[slot], recv_sem=rsem.at[ARRIVALS.index(name)],
                device_id={"tensor": target}, device_id_type=MESH,
            ).start()

        def arrive(dst, *name):
            pltpu.make_async_remote_copy(
                src_ref=dst, dst_ref=dst, send_sem=ssem.at[0], recv_sem=rsem.at[ARRIVALS.index(name)],
                device_id={"tensor": xn}, device_id_type=MESH,
            ).wait_recv()

        def slot_of(q, owner):
            return [v for v in range(LINE) if v != owner].index(q)

        def along(at, cols, kind, q):
            ref = gath.at[at, cols]
            rel = at.start - q * group
            there = lambda v: gath.at[pl.ds(v * group + rel, at.size), cols]
            if p == 0:
                if q == 0:
                    send(ref, there(0), (kind, slot_of(0, 1)), far)
            else:
                if q in (0, 1):
                    send(ref, there(LINE - 1 - q), (kind, slot_of(LINE - 1 - q, 1)), far)
                if q in (1, 2, 3):
                    send(ref, there(q), (kind, slot_of(q, 0)), near)

        def zin(q, kind):
            at = blk(q, 1, 3) if kind == "zc" else blk(q, 0)
            cols = {"za": A, "zb": B}.get(kind, C)
            arrive(gath.at[at, cols], kind, slot_of(q, p))
            along(at, cols, kind, q)

        def first_a(q):
            send(gath.at[blk(q, 0), A], gath.at[blk(q, 1), A], ("xa", q), xn)

        def first_b(q):
            send(gath.at[blk(q, 0), B], gath.at[blk(q, 2), B], ("yb", q), yn)

        def second(q):
            send(gath.at[blk(q, 0), B], gath.at[blk(q, 1), B], ("rest", q), xn)
            send(gath.at[blk(q, 0), A], gath.at[blk(q, 2), A], ("rest", q), yn)

        def pass_a(q):
            zin(q, "za")
            first_a(q)

        def pass_b(q):
            zin(q, "zb")
            first_b(q)
            second(q)

        def relay(q):
            arrive(gath.at[blk(q, 1), A], "xa", q)
            send(gath.at[blk(q, 1), A], gath.at[blk(q, 3), A], ("rest", q), yn)
            arrive(gath.at[blk(q, 2), B], "yb", q)
            send(gath.at[blk(q, 2), B], gath.at[blk(q, 3), B], ("rest", q), xn)

        def start():
            own = gath.at[blk(p, 0), C]
            along(blk(p, 0), A, "za", p)
            first_a(p)
            along(blk(p, 0), B, "zb", p)
            first_b(p)
            along(blk(p, 0), C, "zo", p)
            for r, other in ((1, xn), (2, yn), (3, dn)):
                send(own, gath.at[blk(p, r), C], ("spread", 0), other)
            second(p)

        def spread():
            arrive(gath.at[blk(p, 1, 3), C], "spread", 0)
            along(blk(p, 1, 3), C, "zc", p)

        tile = tile_of(2 * ff, 256)
        wide = tile_of(d, 384)

        def full(q):
            arrive(gath.at[blk(q, 0, 4), A], "rest", q)

        def first(q, n=1):
            at = blk(q, 0, n * PLANE)
            up_to = pl.ds(0, n * group)

            @pl.loop(0, 2 * ff // tile)
            def _(i):
                cols = pl.ds(pl.multiple_of(i * tile, tile), tile)
                gu[up_to, cols] = jnp.dot(gath[at, :], w1[:, cols], preferred_element_type=jnp.float32)

            gate, up = gu[up_to, :ff], gu[up_to, ff:]
            hid[at, :] = (jax.nn.gelu(gate, approximate=True) * up).astype(jnp.bfloat16)

        def last(q, n=1):
            at = blk(q, 0, n * PLANE)

            @pl.loop(0, d // wide)
            def _(i):
                cols = pl.ds(pl.multiple_of(i * wide, wide), wide)
                res = jnp.dot(hid[at, :], w2[:, cols], preferred_element_type=jnp.float32)
                part[at, cols] = res
                sendb[at, cols] = res.astype(jnp.bfloat16)

        if p == 0:
            ways = {1: (far, 0), 2: (far, 1), 3: (me + 3 * step, 2)}
        else:
            ways = {0: (near, 0), 2: (far, 2), 3: (far + step, 1)}
        gather_slots = {0: (), 1: ()} if p == 0 else {0: (), 2: (1,), 3: ()}
        gather_slots[2] = (1,) if p == 1 else ()
        gather_slots[3] = ()
        gather_slots[p] = (0, 1, 2) if p == 0 else (0, 2)

        def turn(q):
            for slot in gather_slots[q]:
                arrive(zc.at[slot], "sc", slot)
                part[blk(q, 0, 4), C] += zc[slot].astype(jnp.float32)
            if gather_slots[q]:
                sendb[blk(q, 0, 4), C] = part[blk(q, 0, 4), C].astype(jnp.bfloat16)
            target, slot = ways[q]
            send(sendb.at[blk(q, 0, 4), C], zc.at[slot], ("sc", slot), target)

        def out_diag(q):
            send(sendb.at[blk(q, 3), A], rda.at[q], ("da", q), xn)
            send(sendb.at[blk(q, 3), B], rdb.at[q], ("db", q), yn)

        def out_side(q):
            send(sendb.at[blk(q, 1), A], rr.at[q, 0, :, A], ("ra", q), xn)
            send(sendb.at[blk(q, 2), B], rr.at[q, 1, :, B], ("rb", q), yn)

        def pass_on(q):
            arrive(rda.at[q], "da", q)
            at = blk(q, 2)
            sendb[at, A] = (part[at, A] + rda[q].astype(jnp.float32)).astype(jnp.bfloat16)
            send(sendb.at[at, A], rr.at[q, 1, :, A], ("ra", q), yn)
            arrive(rdb.at[q], "db", q)
            at = blk(q, 1)
            sendb[at, B] = (part[at, B] + rdb[q].astype(jnp.float32)).astype(jnp.bfloat16)
            send(sendb.at[at, B], rr.at[q, 0, :, B], ("rb", q), xn)

        def settle(q):
            at = blk(q, 0)
            for cols, name, sname in ((A, "ra", "sa"), (B, "rb", "sb")):
                arrive(rr.at[q, :, :, cols], name, q)
                total = part[at, cols] + rr[q, 0, :, cols].astype(jnp.float32) + rr[q, 1, :, cols].astype(jnp.float32)
                if q != p:
                    for slot in gather_slots[q]:
                        arrive(zr.at[slot, :, cols], sname, slot)
                        total += zr[slot, :, cols].astype(jnp.float32)
                    sendb[at, cols] = total.astype(jnp.bfloat16)
                    target, slot = ways[q]
                    send(sendb.at[at, cols], zr.at[slot, :, cols], (sname, slot), target)
                else:
                    part[at, cols] = total

        def share():
            for slot in gather_slots[p]:
                arrive(zc.at[slot], "sc", slot)
                part[blk(p, 0, 4), C] += zc[slot].astype(jnp.float32)
            sendb[blk(p, 1, 3), C] = part[blk(p, 1, 3), C].astype(jnp.bfloat16)
            for r, other in ((1, xn), (2, yn), (3, dn)):
                send(sendb.at[blk(p, r), C], xyc.at[pl.ds((r - 1) * rows, rows)], ("share", 0), other)

        def close():
            at = blk(p, 0)
            for slot in gather_slots[p]:
                for cols, sname in ((A, "sa"), (B, "sb")):
                    arrive(zr.at[slot, :, cols], sname, slot)
                    part[at, cols] += zr[slot, :, cols].astype(jnp.float32)

        def gain():
            arrive(xyc.at[...], "share", 0)
            more = xyc[...].astype(jnp.float32).reshape(3, rows, cw)
            part[blk(p, 0), C] += more[0] + more[1] + more[2]

        def finish():
            total = part[blk(p, 0), :]
            factor = lax.rsqrt(jnp.mean(total * total, axis=1, keepdims=True) + norm_eps)
            post = (total * factor * post_ref[...][None]).astype(jnp.bfloat16)
            stream = stream_ref[...].astype(jnp.float32)
            out_ref[...] = (stream + post.astype(jnp.float32)).astype(jnp.bfloat16)

        def drain():
            for slot, (width, units) in enumerate(sent):
                ref = part.at[pl.ds(0, units * rows // 2), pl.ds(0, width)]
                pltpu.make_async_remote_copy(
                    src_ref=ref, dst_ref=ref, send_sem=ssem.at[slot], recv_sem=rsem.at[0],
                    device_id={"tensor": xn}, device_id_type=MESH,
                ).wait_send()

        gath[blk(p, 0), :] = normed()
        pl.semaphore_wait(barrier, 4 + p)
        S = lambda f, *a: step_of(f, *a)
        if p == 0:
            S(start)
            S(pass_a, 1)
            S(pass_b, 1)
            S(spread)
            S(relay, 0)
            S(pass_a, 2)
            S(pass_b, 2)
            S(relay, 1)
            S(full, 0)
            loads[2].wait()
            loads[3].wait()
            S(first, 0)
            S(pass_a, 3)
            S(pass_b, 3)
            S(relay, 2)
            S(zin, 1, "zo")
            S(zin, 1, "zc")
            S(full, 1)
            S(first, 1)
            S(relay, 3)
            loads[4].wait()
            S(last, 0, 2)
            S(turn, 1)
            S(out_diag, 1)
            S(out_side, 1)
            S(zin, 2, "zo")
            S(zin, 2, "zc")
            S(full, 2)
            S(first, 2)
            S(pass_on, 1)
            S(zin, 3, "zo")
            S(zin, 3, "zc")
            S(full, 3)
            S(first, 3)
            S(last, 2, 2)
            S(turn, 3)
            S(out_diag, 3)
            S(out_diag, 2)
            S(out_side, 3)
            S(turn, 2)
            S(settle, 1)
            S(out_side, 2)
            S(pass_on, 3)
            S(pass_on, 2)
            S(out_diag, 0)
            S(out_side, 0)
            S(settle, 3)
            S(settle, 2)
            S(pass_on, 0)
            loads[5].wait()
            S(share)
            S(settle, 0)
            S(close)
            S(gain)
        else:
            S(start)
            S(pass_a, 0)
            S(pass_a, 2)
            S(pass_b, 0)
            S(pass_b, 2)
            S(zin, 0, "zo")
            S(zin, 2, "zo")
            S(relay, 1)
            S(spread)
            S(pass_a, 3)
            S(pass_b, 3)
            S(zin, 3, "zo")
            S(full, 1)
            loads[2].wait()
            loads[3].wait()
            S(first, 1)
            S(relay, 0)
            S(zin, 0, "zc")
            S(zin, 2, "zc")
            S(relay, 2)
            S(full, 0)
            S(first, 0)
            S(zin, 3, "zc")
            S(relay, 3)
            loads[4].wait()
            S(last, 0, 2)
            S(turn, 0)
            S(out_diag, 0)
            S(out_side, 0)
            S(full, 2)
            S(first, 2)
            S(pass_on, 0)
            S(full, 3)
            S(first, 3)
            S(last, 2, 2)
            S(turn, 3)
            S(out_diag, 3)
            S(out_diag, 2)
            S(out_side, 3)
            S(settle, 0)
            S(out_side, 2)
            S(pass_on, 3)
            S(turn, 2)
            S(pass_on, 2)
            S(out_diag, 1)
            S(out_side, 1)
            S(settle, 3)
            S(settle, 2)
            S(pass_on, 1)
            loads[5].wait()
            S(share)
            S(settle, 1)
            S(close)
            S(gain)
        S(finish)
        S(drain)

    for p in (0, 1):
        pl.when(place == p)(functools.partial(run, p))


def step_of(f, *args):
    with jax.named_scope(f.__name__ + "#" + "_".join(str(a) for a in args)):
        f(*args)


def fused(resid_stream, pre_gain, w_gate, w_up, w_down, post_gain):
    rows, d = resid_stream.shape
    ff = w_gate.shape[1]
    half, cw = cut(d)
    n = PLANE * LINE
    bf, f32, dma = jnp.bfloat16, jnp.float32, pltpu.SemaphoreType.DMA
    hbm = pl.BlockSpec(memory_space=pl.ANY)
    return pl.pallas_call(
        kernel,
        out_shape=pltpu.VMEM((rows, d), bf),
        in_specs=[hbm] * 6,
        out_specs=pl.BlockSpec(memory_space=pltpu.VMEM),
        scratch_shapes=[
            pltpu.VMEM((rows, d), bf),
            pltpu.VMEM((d,), f32),
            pltpu.VMEM((d,), f32),
            pltpu.VMEM((d, 2 * ff), bf),
            pltpu.VMEM((ff, d), bf),
            pltpu.VMEM((n * rows, d), bf),
            pltpu.VMEM((2 * PLANE * rows, 2 * ff), f32),
            pltpu.VMEM((n * rows, ff), bf),
            pltpu.VMEM((n * rows, d), f32),
            pltpu.VMEM((n * rows, d), bf),
            pltpu.VMEM((LINE, rows, half), bf),
            pltpu.VMEM((LINE, rows, half), bf),
            pltpu.VMEM((LINE, 2, rows, d), bf),
            pltpu.VMEM((LINE - 1, rows, 2 * half), bf),
            pltpu.VMEM((LINE - 1, PLANE * rows, cw), bf),
            pltpu.VMEM((3 * rows, cw), bf),
            dma((6,)),
            dma((SENDS,)),
            dma((len(ARRIVALS),)),
        ],
        compiler_params=pltpu.CompilerParams(
            collective_id=0, has_side_effects=True, vmem_limit_bytes=60 * 2**20
        ),
        name="ffn",
    )(resid_stream, pre_gain, w_gate, w_up, w_down, post_gain)


def solution(mesh):
    body = fused if mesh.shape["tensor"] == PLANE * LINE else shards
    return jax.shard_map(
        body,
        mesh=mesh,
        in_specs=(
            P(("dp", "tensor"), None),
            P(),
            P(None, "tensor"),
            P(None, "tensor"),
            P("tensor", None),
            P(),
        ),
        out_specs=P(("dp", "tensor"), None),
        check_vma=False,
    )
```

time: 58 us -> 49.2 us (0.85)
  Pallas kernels: 56.2 us -> 48.3 us
  local copies, waits for them, and re-layouts: 1.58 us -> 0.66 us
    pallas_call x1, Pallas kernels: 56.2 us -> 48.3 us  [fused(): pl.pallas_call(kernel, out_shape=pltpu.VMEM((rows, d), bf), in_specs=[hbm...]
    unnamed x1, local copies, waits for them, and re-layouts: 1.58 us -> 0.66 us
where the time goes in v1:
time: 49.2 us; the launch traced here: 49 us
  Pallas kernels  48.3 us (98%)
  local copies, waits for them, and re-layouts  0.66 us (1%)
    pallas_call x1, Pallas kernels, fused(): pl.pallas_call(kernel, out_shape=pltpu.VMEM((rows, d), bf), in_specs=[hbm...  48.3 us

profile of v1, /device:TPU:0, one launch (start us, length us, event | category | flops | bytes accessed | tf_op | source)
XLA Modules:
  0.0 49.0 jit_solution(8181713407329687393)
XLA Ops:
  0.0 48.3 %ffn.1 = bf16[16,4608]{1,0:T(8,128)(2,1)S(1)} custom-call(bf16[16,4608]{1,0:T(8,128)(2,1)} %stream_hbm.1, f32[4608]{0:T(1024)} %pre_hbm.1, bf16[4608,384]{1,0:T(8,128)(2,1)} %wg_hbm.1, bf16[4608,384]{1,0:T(8,128)(2,1)} %wu_hbm.1, bf16[384,4608]{1,0:T(8,128)(2,1)} %wd_hbm.1, f32[4608]{0:T(1024)} %post_hbm.1), custom_call_target="tpu_custom_call" | custom-call | tf_op jit(solution)/shard_map/ffn/pallas_call | solution.py:449
  48.3 0.7 %copy.8 = bf16[16,4608]{1,0:T(8,128)(2,1)} copy(bf16[16,4608]{1,0:T(8,128)(2,1)S(1)} %ffn.1) | data formatting | bytes 294912

commit v2 on v1

--- a/solution.py
+++ b/solution.py
@@ -54,6 +54,32 @@
 BATCH = 32
 SENDS = 8
 
+PROGRAMS = (
+    (
+        ("start",), ("relay_a", 0), ("pass_a", 1), ("pass_b", 1), ("zo", 1), ("relay_b", 0), ("spread",),
+        ("pass_a", 2), ("relay_a", 1), ("pass_b", 2), ("relay_b", 1), ("zo", 2), ("first", 0), ("zc_", 1),
+        ("relay_a", 2), ("pass_a", 3), ("relay_b", 2), ("pass_b", 3), ("first", 1), ("zo", 3), ("relay_a", 3),
+        ("last", 1), ("zc_", 2), ("relay_b", 3), ("turn", 1), ("out_side", 1), ("out_diag", 1), ("first", 2),
+        ("last", 2), ("zc_", 3), ("turn", 2), ("out_diag", 2), ("out_side", 2), ("first", 3), ("pass_on_b", 1),
+        ("last", 3), ("out_diag", 3), ("turn", 3), ("pass_on_a", 1), ("pass_on_b", 2), ("pass_on_a", 2),
+        ("settle_b", 1), ("pass_on_b", 3), ("pass_on_a", 3), ("out_side", 3), ("settle_a", 1), ("settle_b", 2),
+        ("settle_a", 2), ("last", 0), ("out_diag", 0), ("share",), ("out_side", 0), ("settle_a", 3), ("settle_b", 3),
+        ("pass_on_a", 0), ("pass_on_b", 0), ("gain",), ("settle_a", 0), ("settle_b", 0), ("close",), ("finish",),
+        ("drain",),
+    ),
+    (
+        ("start",), ("pass_a", 0), ("pass_a", 2), ("pass_b", 0), ("pass_b", 2), ("zo", 0), ("zo", 2), ("spread",),
+        ("pass_a", 3), ("relay_a", 0), ("pass_b", 3), ("relay_b", 0), ("zo", 3), ("zc_", 0), ("relay_a", 1),
+        ("relay_b", 2), ("zc_", 2), ("relay_a", 3), ("relay_b", 3), ("relay_b", 1), ("zc_", 3), ("first", 0),
+        ("relay_a", 2), ("last", 0), ("turn", 0), ("out_diag", 0), ("out_side", 0), ("first", 3), ("last", 3),
+        ("turn", 3), ("out_diag", 3), ("out_side", 3), ("first", 2), ("pass_on_b", 0), ("pass_on_a", 0), ("last", 2),
+        ("out_diag", 2), ("first", 1), ("pass_on_a", 3), ("pass_on_b", 3), ("turn", 2), ("last", 1), ("settle_b", 0),
+        ("settle_a", 0), ("out_side", 1), ("out_diag", 1), ("out_side", 2), ("pass_on_a", 2), ("pass_on_b", 2),
+        ("settle_a", 3), ("settle_b", 3), ("share",), ("pass_on_a", 1), ("pass_on_b", 1), ("settle_a", 2),
+        ("settle_b", 2), ("settle_a", 1), ("settle_b", 1), ("gain",), ("close",), ("finish",), ("drain",),
+    ),
+)
+
 
 def kernel(
     stream_hbm, pre_hbm, wg_hbm, wu_hbm, wd_hbm, post_hbm, out_ref,
@@ -116,6 +142,7 @@
 
     def run(p):
         sent = []
+        loaded = set()
 
         def send(src, dst, name, target):
             width = src.shape[-1]
@@ -154,6 +181,12 @@
                 if q in (1, 2, 3):
                     send(ref, there(q), (kind, slot_of(q, 0)), near)
 
+        def zo(q):
+            zin(q, "zo")
+
+        def zc_(q):
+            zin(q, "zc")
+
         def zin(q, kind):
             at = blk(q, 1, 3) if kind == "zc" else blk(q, 0)
             cols = {"za": A, "zb": B}.get(kind, C)
@@ -179,9 +212,11 @@
             first_b(q)
             second(q)
 
-        def relay(q):
+        def relay_a(q):
             arrive(gath.at[blk(q, 1), A], "xa", q)
             send(gath.at[blk(q, 1), A], gath.at[blk(q, 3), A], ("rest", q), yn)
+
+        def relay_b(q):
             arrive(gath.at[blk(q, 2), B], "yb", q)
             send(gath.at[blk(q, 2), B], gath.at[blk(q, 3), B], ("rest", q), xn)
 
@@ -201,12 +236,18 @@
             along(blk(p, 1, 3), C, "zc", p)
 
         tile = tile_of(2 * ff, 256)
-        wide = tile_of(d, 384)
+        wide = tile_of(d, 768)
 
         def full(q):
             arrive(gath.at[blk(q, 0, 4), A], "rest", q)
 
         def first(q, n=1):
+            for v in range(q, q + n):
+                full(v)
+            if "in" not in loaded:
+                loaded.add("in")
+                loads[2].wait()
+                loads[3].wait()
             at = blk(q, 0, n * PLANE)
             up_to = pl.ds(0, n * group)
 
@@ -219,6 +260,9 @@
             hid[at, :] = (jax.nn.gelu(gate, approximate=True) * up).astype(jnp.bfloat16)
 
         def last(q, n=1):
+            if "out" not in loaded:
+                loaded.add("out")
+                loads[4].wait()
             at = blk(q, 0, n * PLANE)
 
             @pl.loop(0, d // wide)
@@ -254,30 +298,37 @@
             send(sendb.at[blk(q, 1), A], rr.at[q, 0, :, A], ("ra", q), xn)
             send(sendb.at[blk(q, 2), B], rr.at[q, 1, :, B], ("rb", q), yn)
 
-        def pass_on(q):
+        def pass_on_a(q):
             arrive(rda.at[q], "da", q)
             at = blk(q, 2)
             sendb[at, A] = (part[at, A] + rda[q].astype(jnp.float32)).astype(jnp.bfloat16)
             send(sendb.at[at, A], rr.at[q, 1, :, A], ("ra", q), yn)
+
+        def pass_on_b(q):
             arrive(rdb.at[q], "db", q)
             at = blk(q, 1)
             sendb[at, B] = (part[at, B] + rdb[q].astype(jnp.float32)).astype(jnp.bfloat16)
             send(sendb.at[at, B], rr.at[q, 0, :, B], ("rb", q), xn)
 
-        def settle(q):
+        def settle(q, cols, name, sname):
             at = blk(q, 0)
-            for cols, name, sname in ((A, "ra", "sa"), (B, "rb", "sb")):
-                arrive(rr.at[q, :, :, cols], name, q)
-                total = part[at, cols] + rr[q, 0, :, cols].astype(jnp.float32) + rr[q, 1, :, cols].astype(jnp.float32)
-                if q != p:
-                    for slot in gather_slots[q]:
-                        arrive(zr.at[slot, :, cols], sname, slot)
-                        total += zr[slot, :, cols].astype(jnp.float32)
-                    sendb[at, cols] = total.astype(jnp.bfloat16)
-                    target, slot = ways[q]
-                    send(sendb.at[at, cols], zr.at[slot, :, cols], (sname, slot), target)
-                else:
-                    part[at, cols] = total
+            arrive(rr.at[q, :, :, cols], name, q)
+            total = part[at, cols] + rr[q, 0, :, cols].astype(jnp.float32) + rr[q, 1, :, cols].astype(jnp.float32)
+            if q == p:
+                part[at, cols] = total
+                return
+            for slot in gather_slots[q]:
+                arrive(zr.at[slot, :, cols], sname, slot)
+                total += zr[slot, :, cols].astype(jnp.float32)
+            sendb[at, cols] = total.astype(jnp.bfloat16)
+            target, slot = ways[q]
+            send(sendb.at[at, cols], zr.at[slot, :, cols], (sname, slot), target)
+
+        def settle_a(q):
+            settle(q, A, "ra", "sa")
+
+        def settle_b(q):
+            settle(q, B, "rb", "sb")
 
         def share():
             for slot in gather_slots[p]:
@@ -300,6 +351,7 @@
             part[blk(p, 0), C] += more[0] + more[1] + more[2]
 
         def finish():
+            loads[5].wait()
             total = part[blk(p, 0), :]
             factor = lax.rsqrt(jnp.mean(total * total, axis=1, keepdims=True) + norm_eps)
             post = (total * factor * post_ref[...][None]).astype(jnp.bfloat16)
@@ -316,119 +368,12 @@
 
         gath[blk(p, 0), :] = normed()
         pl.semaphore_wait(barrier, 4 + p)
-        S = lambda f, *a: step_of(f, *a)
-        if p == 0:
-            S(start)
-            S(pass_a, 1)
-            S(pass_b, 1)
-            S(spread)
-            S(relay, 0)
-            S(pass_a, 2)
-            S(pass_b, 2)
-            S(relay, 1)
-            S(full, 0)
-            loads[2].wait()
-            loads[3].wait()
-            S(first, 0)
-            S(pass_a, 3)
-            S(pass_b, 3)
-            S(relay, 2)
-            S(zin, 1, "zo")
-            S(zin, 1, "zc")
-            S(full, 1)
-            S(first, 1)
-            S(relay, 3)
-            loads[4].wait()
-            S(last, 0, 2)
-            S(turn, 1)
-            S(out_diag, 1)
-            S(out_side, 1)
-            S(zin, 2, "zo")
-            S(zin, 2, "zc")
-            S(full, 2)
-            S(first, 2)
-            S(pass_on, 1)
-            S(zin, 3, "zo")
-            S(zin, 3, "zc")
-            S(full, 3)
-            S(first, 3)
-            S(last, 2, 2)
-            S(turn, 3)
-            S(out_diag, 3)
-            S(out_diag, 2)
-            S(out_side, 3)
-            S(turn, 2)
-            S(settle, 1)
-            S(out_side, 2)
-            S(pass_on, 3)
-            S(pass_on, 2)
-            S(out_diag, 0)
-            S(out_side, 0)
-            S(settle, 3)
-            S(settle, 2)
-            S(pass_on, 0)
-            loads[5].wait()
-            S(share)
-            S(settle, 0)
-            S(close)
-            S(gain)
-        else:
-            S(start)
-            S(pass_a, 0)
-            S(pass_a, 2)
-            S(pass_b, 0)
-            S(pass_b, 2)
-            S(zin, 0, "zo")
-            S(zin, 2, "zo")
-            S(relay, 1)
-            S(spread)
-            S(pass_a, 3)
-            S(pass_b, 3)
-            S(zin, 3, "zo")
-            S(full, 1)
-            loads[2].wait()
-            loads[3].wait()
-            S(first, 1)
-            S(relay, 0)
-            S(zin, 0, "zc")
-            S(zin, 2, "zc")
-            S(relay, 2)
-            S(full, 0)
-            S(first, 0)
-            S(zin, 3, "zc")
-            S(relay, 3)
-            loads[4].wait()
-            S(last, 0, 2)
-            S(turn, 0)
-            S(out_diag, 0)
-            S(out_side, 0)
-            S(full, 2)
-            S(first, 2)
-            S(pass_on, 0)
-            S(full, 3)
-            S(first, 3)
-            S(last, 2, 2)
-            S(turn, 3)
-            S(out_diag, 3)
-            S(out_diag, 2)
-            S(out_side, 3)
-            S(settle, 0)
-            S(out_side, 2)
-            S(pass_on, 3)
-            S(turn, 2)
-            S(pass_on, 2)
-            S(out_diag, 1)
-            S(out_side, 1)
-            S(settle, 3)
-            S(settle, 2)
-            S(pass_on, 1)
-            loads[5].wait()
-            S(share)
-            S(settle, 1)
-            S(close)
-            S(gain)
-        S(finish)
-        S(drain)
+        steps = {f.__name__: f for f in (
+            start, spread, share, close, gain, finish, drain, pass_a, pass_b, zo, zc_, relay_a, relay_b, first, last,
+            turn, out_diag, out_side, pass_on_a, pass_on_b, settle_a, settle_b,
+        )}
+        for name, *args in PROGRAMS[p]:
+            step_of(steps[name], *args)
 
     for p in (0, 1):
         pl.when(place == p)(functools.partial(run, p))

time: 49.2 us -> 44.5 us (0.904)
  Pallas kernels: 48.3 us -> 43.7 us
    pallas_call x1, Pallas kernels: 48.3 us -> 43.7 us  [fused(): pl.pallas_call(kernel, out_shape=pltpu.VMEM((rows, d), bf), in_specs=[hbm...]
where the time goes in v2:
time: 44.5 us; the launch traced here: 44.4 us
  Pallas kernels  43.7 us (98%)
  local copies, waits for them, and re-layouts  0.66 us (1%)
    pallas_call x1, Pallas kernels, fused(): pl.pallas_call(kernel, out_shape=pltpu.VMEM((rows, d), bf), in_specs=[hbm...  43.7 us

profile of v2, /device:TPU:0, one launch (start us, length us, event | category | flops | bytes accessed | tf_op | source)
XLA Modules:
  0.0 44.4 jit_solution(973205049226136109)
XLA Ops:
  0.0 43.7 %ffn.1 = bf16[16,4608]{1,0:T(8,128)(2,1)S(1)} custom-call(bf16[16,4608]{1,0:T(8,128)(2,1)} %stream_hbm.1, f32[4608]{0:T(1024)} %pre_hbm.1, bf16[4608,384]{1,0:T(8,128)(2,1)} %wg_hbm.1, bf16[4608,384]{1,0:T(8,128)(2,1)} %wu_hbm.1, bf16[384,4608]{1,0:T(8,128)(2,1)} %wd_hbm.1, f32[4608]{0:T(1024)} %post_hbm.1), custom_call_target="tpu_custom_call" | custom-call | tf_op jit(solution)/shard_map/ffn/pallas_call | solution.py:394
  43.7 0.7 %copy.8 = bf16[16,4608]{1,0:T(8,128)(2,1)} copy(bf16[16,4608]{1,0:T(8,128)(2,1)S(1)} %ffn.1) | data formatting | bytes 294912

commit v3 on v2

v3 whole, which is shorter than its diff:
```python
import functools

import jax
import jax.numpy as jnp
from jax import lax
from jax.experimental import pallas as pl
from jax.experimental.pallas import tpu as pltpu
from jax.sharding import PartitionSpec as P

norm_eps = 1e-06
SIDE = 2
PLANE = SIDE * SIDE
OUT_END, OUT_MID, BACK_END, BACK_MID = 7, 3, 4, 4
LINE = 4
MESH = pl.DeviceIdType.MESH


def shards(resid_stream, pre_gain, w_gate, w_up, w_down, post_gain):
    stream = resid_stream.astype(jnp.float32)
    local_norm = stream * lax.rsqrt(jnp.mean(stream * stream, axis=1, keepdims=True) + norm_eps)
    normed = (local_norm * pre_gain).astype(jnp.bfloat16)
    row_piece = lax.all_gather(normed, "tensor", axis=0, tiled=True)
    gate_out = jnp.dot(row_piece, w_gate, preferred_element_type=jnp.float32)
    up_out = jnp.dot(row_piece, w_up, preferred_element_type=jnp.float32)
    hidden = (jax.nn.gelu(gate_out, approximate=True) * up_out).astype(jnp.bfloat16)
    block_rows = lax.psum_scatter(
        jnp.dot(hidden, w_down, preferred_element_type=jnp.float32),
        "tensor",
        scatter_dimension=0,
        tiled=True,
    )
    row_factor = lax.rsqrt(jnp.mean(block_rows * block_rows, axis=1, keepdims=True) + norm_eps)
    post = (block_rows * row_factor * post_gain).astype(jnp.bfloat16)
    post = lax.optimization_barrier(post)
    return (stream + post.astype(jnp.float32)).astype(jnp.bfloat16)


def cut(d, turned):
    lanes = d // 128
    most = 2 * (turned * lanes // 36) + lanes % 2
    return (lanes - most) // 2 * 128, most * 128


def parts(d, turned):
    half, cw = cut(d, turned)
    return pl.ds(0, half), pl.ds(half, half), pl.ds(2 * half, cw)


BATCH = 32
WAYS = 5
E3_AB, E3_C, I3_AB, I3_C = True, True, True, True
KIND = ("zo", "z1", "z2", "z3")
ARRIVALS = [
    *((name, q) for name in ("xa", "yb", "rest", "da", "db", "ra", "rb") for q in range(LINE)),
    *((name, j) for name in ("za", "zb", "zo", "z1", "z2", "z3") for j in range(LINE - 1)),
    *((name, i) for name in ("sa", "sb", "sc") for i in range(WAYS)),
    *(("spread", r) for r in range(1, PLANE)),
    ("share", 0),
]
SENDS = 12


def kernel(
    stream_hbm, pre_hbm, wg_hbm, wu_hbm, wd_hbm, post_hbm, out_ref,
    stream_ref, pre_ref, post_ref, w1, w2, gath, gu, hid, part, sendb, rd, rr, zr, zrc, xyc,
    lsem, ssem, rsem,
):
    rows, d = stream_ref.shape
    ff = wg_hbm.shape[1]
    group = PLANE * rows
    out_cols, back_cols = ([parts(d, v) for v in (e, m, m, e)] for e, m in ((OUT_END, OUT_MID), (BACK_END, BACK_MID)))

    me = lax.axis_index("tensor")
    x = lax.rem(me, SIDE)
    y = lax.rem(lax.div(me, SIDE), SIDE)
    z = lax.div(me, PLANE)
    sx = 1 - 2 * x
    sy = SIDE * (1 - 2 * y)
    xn, yn, dn = me + sx, me + sy, me + sx + sy
    flip = lax.div(z, LINE // 2)
    step = PLANE * (1 - 2 * flip)
    place = z + flip * (LINE - 1 - 2 * z)
    far, near = me + step, me - step

    barrier = pltpu.get_barrier_semaphore()
    for other in (xn, yn, dn, far):
        pl.semaphore_signal(barrier, inc=1, device_id={"tensor": other}, device_id_type=MESH)

    @pl.when(place == 1)
    def _():
        pl.semaphore_signal(barrier, inc=1, device_id={"tensor": near}, device_id_type=MESH)

    loads = [
        pltpu.make_async_copy(src, dst, lsem.at[i])
        for i, (src, dst) in enumerate(
            (
                (stream_hbm, stream_ref),
                (pre_hbm, pre_ref),
                (wg_hbm, w1.at[:, pl.ds(0, ff)]),
                (wu_hbm, w1.at[:, pl.ds(ff, ff)]),
                (wd_hbm, w2),
                (post_hbm, post_ref),
            )
        )
    ]
    for load in loads:
        load.start()
    loads[0].wait()
    loads[1].wait()

    def blk(q, r, n=1):
        return pl.ds((q * PLANE + r) * rows, n * rows)

    def normed():
        stream = stream_ref[...].astype(jnp.float32)
        scale = lax.rsqrt(jnp.mean(stream * stream, axis=1, keepdims=True) + norm_eps)
        return (stream * scale * pre_ref[...][None]).astype(jnp.bfloat16)

    def run(v):
        p = min(v, LINE - 1 - v)
        sent = []
        loaded, gated = set(), set()

        def send(src, dst, name, target):
            width = src.shape[-1]
            units = src.size // (rows * width) if hasattr(src, "size") else src.shape[0] // rows
            for slot, entry in enumerate(sent):
                if entry[0] == width and entry[1] + units <= BATCH:
                    entry[1] += units
                    break
            else:
                slot = len(sent)
                sent.append([width, units])
            pltpu.make_async_remote_copy(
                src_ref=src, dst_ref=dst, send_sem=ssem.at[slot], recv_sem=rsem.at[ARRIVALS.index(name)],
                device_id={"tensor": target}, device_id_type=MESH,
            ).start()

        def arrive(dst, *name):
            pltpu.make_async_remote_copy(
                src_ref=dst, dst_ref=dst, send_sem=ssem.at[0], recv_sem=rsem.at[ARRIVALS.index(name)],
                device_id={"tensor": xn}, device_id_type=MESH,
            ).wait_recv()

        def slot_of(q, owner):
            return [v for v in range(LINE) if v != owner].index(q)

        def along(at, cols, kind, q):
            ref = gath.at[at, cols]
            rel = at.start - q * group
            there = lambda v: gath.at[pl.ds(v * group + rel, at.size), cols]
            if p == 0:
                if q == 0:
                    send(ref, there(0), (kind, slot_of(0, 1)), far)
            else:
                if q in (0, 1):
                    send(ref, there(LINE - 1 - q), (kind, slot_of(LINE - 1 - q, 1)), far)
                if q in (1, 2, 3):
                    send(ref, there(q), (kind, slot_of(q, 0)), near)

        def zo(q):
            zin(q, "zo")

        def zc(q, r):
            zin(q, KIND[r])

        def zin(q, kind):
            at = blk(q, int(kind[1])) if kind[1].isdigit() else blk(q, 0)
            cols = out_cols[q][{"za": 0, "zb": 1}.get(kind, 2)]
            arrive(gath.at[at, cols], kind, slot_of(q, p))
            along(at, cols, kind, q)

        def first_a(q):
            A = out_cols[q][0]
            send(gath.at[blk(q, 0), A], gath.at[blk(q, 1), A], ("xa", q), xn)

        def first_b(q):
            B = out_cols[q][1]
            send(gath.at[blk(q, 0), B], gath.at[blk(q, 2), B], ("yb", q), yn)

        def second(q):
            A, B, _ = out_cols[q]
            send(gath.at[blk(q, 0), B], gath.at[blk(q, 1), B], ("rest", q), xn)
            send(gath.at[blk(q, 0), A], gath.at[blk(q, 2), A], ("rest", q), yn)

        def pass_a(q):
            zin(q, "za")
            first_a(q)

        def pass_b(q):
            zin(q, "zb")
            first_b(q)
            second(q)

        def relay_a(q):
            A = out_cols[q][0]
            arrive(gath.at[blk(q, 1), A], "xa", q)
            send(gath.at[blk(q, 1), A], gath.at[blk(q, 3), A], ("rest", q), yn)

        def relay_b(q):
            B = out_cols[q][1]
            arrive(gath.at[blk(q, 2), B], "yb", q)
            send(gath.at[blk(q, 2), B], gath.at[blk(q, 3), B], ("rest", q), xn)

        def start():
            A, B, C = out_cols[p]
            own = gath.at[blk(p, 0), C]
            along(blk(p, 0), A, "za", p)
            first_a(p)
            along(blk(p, 0), B, "zb", p)
            first_b(p)
            along(blk(p, 0), C, "zo", p)
            for r, other in ((1, xn), (2, yn), (3, dn)):
                send(own, gath.at[blk(p, r), C], ("spread", r), other)
            second(p)

        def spread(r):
            C = out_cols[p][2]
            arrive(gath.at[blk(p, r), C], "spread", r)
            along(blk(p, r), C, KIND[r], p)

        def full(q):
            arrive(gath.at[blk(q, 0, 4), out_cols[q][0]], "rest", q)

        def first(q, n=1):
            for v in range(q, q + n):
                full(v)
            if "in" not in loaded:
                loaded.add("in")
                loads[2].wait()
                loads[3].wait()
            beside = [v for v in (q - 1, q + 1) if n == 1 and v in gated]
            low, m = (min(q, beside[0]), 2) if beside else (q, n)
            gated.update(range(q, q + n))
            gu[blk(0, 0, m * PLANE), :] = jnp.dot(
                gath[blk(low, 0, m * PLANE), :], w1[...], preferred_element_type=jnp.float32
            )
            own = blk(q - low, 0, n * PLANE)
            gate, up = gu[own, :ff], gu[own, ff:]
            hid[blk(q, 0, n * PLANE), :] = (jax.nn.gelu(gate, approximate=True) * up).astype(jnp.bfloat16)

        def last(q, n=1):
            if "out" not in loaded:
                loaded.add("out")
                loads[4].wait()
            at = blk(q, 0, n * PLANE)

            res = jnp.dot(hid[at, :], w2[...], preferred_element_type=jnp.float32)
            part[at, :] = res
            sendb[at, :] = res.astype(jnp.bfloat16)

        def way(q, end_direct, inner_direct):
            if p == 0:
                return {1: (far, 0), 2: (far, 1), 3: (me + 3 * step, 2) if end_direct else (far, 3)}[q]
            return {0: (near, 0), 2: (far, 2), 3: (far + step, 1) if inner_direct else (far, 4)}[q]

        def added(q, end_direct, inner_direct):
            if q == p:
                return (0, 2) if p else (0, *((1,) if inner_direct else ()), *((2,) if end_direct else ()))
            if p == 0:
                return ()
            return {0: () if inner_direct else (4,), 2: (1,), 3: () if end_direct else (3,)}[q]

        def line_sum(q, at, cols):
            for slot in added(q, E3_C, I3_C):
                arrive(zrc.at[slot, :, pl.ds(0, cols.size)], "sc", slot)
                part[at, cols] += zrc[slot, :, :cols.size].astype(jnp.float32)

        def turn(q):
            at, C = blk(q, 0, 4), back_cols[q][2]
            line_sum(q, at, C)
            if added(q, E3_C, I3_C):
                sendb[at, C] = part[at, C].astype(jnp.bfloat16)
            target, slot = way(q, E3_C, I3_C)
            send(sendb.at[at, C], zrc.at[slot, :, pl.ds(0, C.size)], ("sc", slot), target)

        def out_diag(q):
            A, B, _ = back_cols[q]
            send(sendb.at[blk(q, 3), A], rd.at[q, :, A], ("da", q), xn)
            send(sendb.at[blk(q, 3), B], rd.at[q, :, B], ("db", q), yn)

        def out_side(q):
            A, B, _ = back_cols[q]
            send(sendb.at[blk(q, 1), A], rr.at[q, 0, :, A], ("ra", q), xn)
            send(sendb.at[blk(q, 2), B], rr.at[q, 1, :, B], ("rb", q), yn)

        def pass_on_a(q):
            at, A = blk(q, 2), back_cols[q][0]
            arrive(rd.at[q, :, A], "da", q)
            sendb[at, A] = (part[at, A] + rd[q, :, A].astype(jnp.float32)).astype(jnp.bfloat16)
            send(sendb.at[at, A], rr.at[q, 1, :, A], ("ra", q), yn)

        def pass_on_b(q):
            at, B = blk(q, 1), back_cols[q][1]
            arrive(rd.at[q, :, B], "db", q)
            sendb[at, B] = (part[at, B] + rd[q, :, B].astype(jnp.float32)).astype(jnp.bfloat16)
            send(sendb.at[at, B], rr.at[q, 0, :, B], ("rb", q), xn)

        def settle(q, cols, name, sname):
            at = blk(q, 0)
            arrive(rr.at[q, :, :, cols], name, q)
            total = part[at, cols] + rr[q, 0, :, cols].astype(jnp.float32) + rr[q, 1, :, cols].astype(jnp.float32)
            if q == p:
                part[at, cols] = total
                return
            for slot in added(q, E3_AB, I3_AB):
                arrive(zr.at[slot, :, cols], sname, slot)
                total += zr[slot, :, cols].astype(jnp.float32)
            sendb[at, cols] = total.astype(jnp.bfloat16)
            target, slot = way(q, E3_AB, I3_AB)
            send(sendb.at[at, cols], zr.at[slot, :, cols], (sname, slot), target)

        def settle_a(q):
            settle(q, back_cols[q][0], "ra", "sa")

        def settle_b(q):
            settle(q, back_cols[q][1], "rb", "sb")

        def share():
            C = back_cols[p][2]
            line_sum(p, blk(p, 0, 4), C)
            sendb[blk(p, 1, 3), C] = part[blk(p, 1, 3), C].astype(jnp.bfloat16)
            for r, other in ((1, xn), (2, yn), (3, dn)):
                place_of = xyc.at[pl.ds((r - 1) * rows, rows), pl.ds(0, C.size)]
                send(sendb.at[blk(p, r), C], place_of, ("share", 0), other)

        def close():
            at = blk(p, 0)
            for slot in added(p, E3_AB, I3_AB):
                for cols, sname in zip(back_cols[p], ("sa", "sb")):
                    arrive(zr.at[slot, :, cols], sname, slot)
                    part[at, cols] += zr[slot, :, cols].astype(jnp.float32)

        def gain():
            C = back_cols[p][2]
            arrive(xyc.at[:, pl.ds(0, C.size)], "share", 0)
            more = xyc[:, :C.size].astype(jnp.float32).reshape(3, rows, C.size)
            part[blk(p, 0), C] += more[0] + more[1] + more[2]

        def finish():
            loads[5].wait()
            total = part[blk(p, 0), :]
            factor = lax.rsqrt(jnp.mean(total * total, axis=1, keepdims=True) + norm_eps)
            post = (total * factor * post_ref[...][None]).astype(jnp.bfloat16)
            stream = stream_ref[...].astype(jnp.float32)
            out_ref[...] = (stream + post.astype(jnp.float32)).astype(jnp.bfloat16)

        def drain():
            for slot, (width, units) in enumerate(sent):
                ref = part.at[pl.ds(0, units * rows // 2), pl.ds(0, width)]
                pltpu.make_async_remote_copy(
                    src_ref=ref, dst_ref=ref, send_sem=ssem.at[slot], recv_sem=rsem.at[0],
                    device_id={"tensor": xn}, device_id_type=MESH,
                ).wait_send()

        gath[blk(p, 0), :] = normed()
        pl.semaphore_wait(barrier, 4 + p)
        programs = ((
                (start,), (relay_a, 0), (pass_a, 1), (spread, 2), (pass_b, 1), (zo, 1), (spread, 3), (pass_a, 2),
                (relay_a, 1), (zc, 1, 2), (zc, 1, 1), (relay_b, 1), (spread, 1), (relay_b, 0), (pass_b, 2),
                (zc, 1, 3), (zo, 2), (relay_a, 2), (pass_a, 3), (first, 1, 1), (zc, 2, 2), (zc, 2, 1), (relay_b, 2),
                (last, 1, 1), (pass_b, 3), (turn, 1), (out_diag, 1), (first, 0, 1), (zc, 2, 3), (zo, 3), (relay_a, 3),
                (last, 0, 1), (zc, 3, 1), (out_side, 0), (first, 2, 1), (zc, 3, 2), (relay_b, 3), (last, 2, 1),
                (zc, 3, 3), (turn, 2), (out_side, 2), (pass_on_a, 1), (out_diag, 2), (out_side, 1), (pass_on_b, 1),
                (first, 3, 1), (last, 3, 1), (out_diag, 3), (turn, 3), (pass_on_a, 2), (settle_a, 1), (pass_on_b, 2),
                (settle_b, 1), (pass_on_a, 3), (out_side, 3), (out_diag, 0), (pass_on_b, 3), (settle_b, 2),
                (settle_a, 2), (share,), (settle_a, 3), (pass_on_a, 0), (pass_on_b, 0), (settle_b, 3), (settle_a, 0),
                (gain,), (settle_b, 0), (close,), (finish,), (drain,),
            ), (
                (start,), (pass_a, 0), (relay_a, 1), (pass_a, 2), (pass_b, 0), (spread, 2), (spread, 1), (zo, 0),
                (pass_b, 2), (spread, 3), (zo, 2), (relay_a, 0), (pass_a, 3), (zc, 2, 1), (zc, 0, 2), (zc, 2, 2),
                (relay_a, 2), (relay_b, 0), (pass_b, 3), (zc, 0, 3), (zo, 3), (relay_b, 2), (zc, 2, 3), (relay_a, 3),
                (zc, 3, 1), (zc, 0, 1), (first, 0, 1), (zc, 3, 2), (last, 0, 1), (zc, 3, 3), (turn, 0), (relay_b, 3),
                (relay_b, 1), (out_diag, 0), (out_side, 0), (first, 2, 1), (last, 2, 1), (out_diag, 2), (out_side, 2),
                (first, 3, 1), (pass_on_b, 0), (last, 3, 1), (turn, 3), (out_diag, 3), (out_side, 3), (first, 1, 1),
                (pass_on_b, 2), (pass_on_a, 0), (last, 1, 1), (out_side, 1), (out_diag, 1), (pass_on_a, 2),
                (pass_on_b, 3), (turn, 2), (settle_b, 0), (settle_a, 0), (pass_on_a, 3), (pass_on_b, 1),
                (settle_a, 3), (share,), (pass_on_a, 1), (settle_b, 2), (settle_b, 3), (settle_a, 2), (settle_b, 1),
                (settle_a, 1), (gain,), (close,), (finish,), (drain,),
            ), (
                (start,), (pass_a, 2), (pass_a, 0), (relay_a, 1), (spread, 1), (spread, 2), (pass_b, 0), (pass_b, 2),
                (zo, 2), (zo, 0), (pass_a, 3), (spread, 3), (pass_b, 3), (zc, 2, 2), (zc, 2, 1), (zc, 0, 1),
                (relay_a, 0), (relay_b, 0), (zo, 3), (zc, 0, 2), (zc, 2, 3), (zc, 0, 3), (relay_b, 2), (zc, 3, 2),
                (relay_a, 3), (zc, 3, 3), (relay_b, 3), (relay_b, 1), (first, 0, 1), (relay_a, 2), (zc, 3, 1),
                (last, 0, 1), (out_diag, 0), (turn, 0), (out_side, 0), (first, 3, 1), (last, 3, 1), (turn, 3),
                (out_diag, 3), (out_side, 3), (first, 1, 1), (pass_on_a, 0), (pass_on_b, 0), (last, 1, 1),
                (out_diag, 1), (first, 2, 1), (pass_on_a, 3), (last, 2, 1), (out_diag, 2), (pass_on_b, 3),
                (out_side, 1), (turn, 2), (settle_b, 0), (out_side, 2), (settle_a, 0), (pass_on_a, 1), (pass_on_b, 1),
                (pass_on_a, 2), (settle_a, 3), (settle_b, 3), (share,), (pass_on_b, 2), (settle_b, 1), (settle_a, 1),
                (settle_a, 2), (settle_b, 2), (gain,), (close,), (finish,), (drain,),
            ), (
                (start,), (relay_a, 0), (pass_a, 1), (spread, 1), (spread, 2), (pass_b, 1), (zo, 1), (relay_b, 0),
                (pass_a, 2), (spread, 3), (zc, 1, 1), (zc, 1, 2), (relay_a, 1), (pass_b, 2), (relay_b, 1), (zo, 2),
                (first, 0, 1), (pass_a, 3), (zc, 1, 3), (relay_a, 2), (pass_b, 3), (zc, 2, 2), (relay_b, 2),
                (zc, 2, 1), (zo, 3), (first, 1, 1), (zc, 2, 3), (relay_a, 3), (last, 1, 1), (zc, 3, 2), (relay_b, 3),
                (turn, 1), (out_side, 1), (out_diag, 1), (zc, 3, 3), (first, 2, 1), (last, 2, 1), (zc, 3, 1),
                (out_diag, 2), (out_side, 2), (turn, 2), (first, 3, 1), (pass_on_b, 1), (last, 3, 1), (out_diag, 3),
                (turn, 3), (pass_on_a, 1), (pass_on_b, 2), (pass_on_a, 2), (pass_on_b, 3), (settle_b, 1),
                (settle_a, 1), (pass_on_a, 3), (out_side, 3), (settle_a, 2), (last, 0, 1), (out_diag, 0),
                (settle_b, 2), (out_side, 0), (settle_a, 3), (settle_b, 3), (pass_on_a, 0), (share,), (pass_on_b, 0),
                (settle_a, 0), (gain,), (settle_b, 0), (close,), (finish,), (drain,),
            ))
        for f, *args in programs[v]:
            with jax.named_scope("#".join([f.__name__, *map(str, args)])):
                f(*args)

    for v in range(LINE):
        pl.when(z == v)(functools.partial(run, v))


def fused(resid_stream, pre_gain, w_gate, w_up, w_down, post_gain):
    rows, d = resid_stream.shape
    ff = w_gate.shape[1]
    cw = max(cut(d, v)[1] for v in (BACK_END, BACK_MID))
    n = PLANE * LINE
    bf, f32, dma = jnp.bfloat16, jnp.float32, pltpu.SemaphoreType.DMA
    hbm = pl.BlockSpec(memory_space=pl.ANY)
    return pl.pallas_call(
        kernel,
        out_shape=pltpu.VMEM((rows, d), bf),
        in_specs=[hbm] * 6,
        out_specs=pl.BlockSpec(memory_space=pltpu.VMEM),
        scratch_shapes=[
            pltpu.VMEM((rows, d), bf),
            pltpu.VMEM((d,), f32),
            pltpu.VMEM((d,), f32),
            pltpu.VMEM((d, 2 * ff), bf),
            pltpu.VMEM((ff, d), bf),
            pltpu.VMEM((n * rows, d), bf),
            pltpu.VMEM((n * rows, 2 * ff), f32),
            pltpu.VMEM((n * rows, ff), bf),
            pltpu.VMEM((n * rows, d), f32),
            pltpu.VMEM((n * rows, d), bf),
            pltpu.VMEM((LINE, rows, d), bf),
            pltpu.VMEM((LINE, 2, rows, d), bf),
            pltpu.VMEM((WAYS, rows, d), bf),
            pltpu.VMEM((WAYS, PLANE * rows, cw), bf),
            pltpu.VMEM((3 * rows, cw), bf),
            dma((6,)),
            dma((SENDS,)),
            dma((len(ARRIVALS),)),
        ],
        compiler_params=pltpu.CompilerParams(
            collective_id=0, has_side_effects=True, vmem_limit_bytes=60 * 2**20
        ),
        name="ffn",
    )(resid_stream, pre_gain, w_gate, w_up, w_down, post_gain)


def solution(mesh):
    body = fused if mesh.shape["tensor"] == PLANE * LINE else shards
    return jax.shard_map(
        body,
        mesh=mesh,
        in_specs=(
            P(("dp", "tensor"), None),
            P(),
            P(None, "tensor"),
            P(None, "tensor"),
            P("tensor", None),
            P(),
        ),
        out_specs=P(("dp", "tensor"), None),
        check_vma=False,
    )
```

time: 44.5 us -> 43.9 us (0.987)
  Pallas kernels: 43.7 us -> 43.1 us
    pallas_call x1, Pallas kernels: 43.7 us -> 43.1 us  [fused(): pl.pallas_call(kernel, out_shape=pltpu.VMEM((rows, d), bf), in_specs=[hbm...]
where the time goes in v3:
time: 43.9 us; the launch traced here: 43.8 us
  Pallas kernels  43.1 us (98%)
  local copies, waits for them, and re-layouts  0.66 us (2%)
    pallas_call x1, Pallas kernels, fused(): pl.pallas_call(kernel, out_shape=pltpu.VMEM((rows, d), bf), in_specs=[hbm...  43.1 us

profile of v3, /device:TPU:0, one launch (start us, length us, event | category | flops | bytes accessed | tf_op | source)
XLA Modules:
  0.0 43.8 jit_solution(2209273925825154383)
XLA Ops:
  0.0 43.1 %ffn.1 = bf16[16,4608]{1,0:T(8,128)(2,1)S(1)} custom-call(bf16[16,4608]{1,0:T(8,128)(2,1)} %stream_hbm.1, f32[4608]{0:T(1024)} %pre_hbm.1, bf16[4608,384]{1,0:T(8,128)(2,1)} %wg_hbm.1, bf16[4608,384]{1,0:T(8,128)(2,1)} %wu_hbm.1, bf16[384,4608]{1,0:T(8,128)(2,1)} %wd_hbm.1, f32[4608]{0:T(1024)} %post_hbm.1), custom_call_target="tpu_custom_call" | custom-call | tf_op jit(solution)/shard_map/ffn/pallas_call | solution.py:418
  43.1 0.7 %copy.8 = bf16[16,4608]{1,0:T(8,128)(2,1)} copy(bf16[16,4608]{1,0:T(8,128)(2,1)S(1)} %ffn.1) | data formatting | bytes 294912

commit v4 on v3

--- a/solution.py
+++ b/solution.py
@@ -47,7 +47,7 @@
 
 
 BATCH = 32
-WAYS = 5
+WAYS = 3
 E3_AB, E3_C, I3_AB, I3_C = True, True, True, True
 KIND = ("zo", "z1", "z2", "z3")
 ARRIVALS = [
@@ -57,7 +57,7 @@
     *(("spread", r) for r in range(1, PLANE)),
     ("share", 0),
 ]
-SENDS = 12
+SENDS = 6
 
 
 def kernel(
@@ -404,7 +404,7 @@
             with jax.named_scope("#".join([f.__name__, *map(str, args)])):
                 f(*args)
 
-    for v in range(LINE):
+    for v in reversed(range(LINE)):
         pl.when(z == v)(functools.partial(run, v))
 
 

time: 43.9 us -> 43.4 us (0.989)
  Pallas kernels: 43.1 us -> 42.3 us
    pallas_call x1, Pallas kernels: 43.1 us -> 42.3 us  [fused(): pl.pallas_call(kernel, out_shape=pltpu.VMEM((rows, d), bf), in_specs=[hbm...]
where the time goes in v4:
time: 43.4 us; the launch traced here: 43 us
  Pallas kernels  42.3 us (97%)
  local copies, waits for them, and re-layouts  0.66 us (2%)
    pallas_call x1, Pallas kernels, fused(): pl.pallas_call(kernel, out_shape=pltpu.VMEM((rows, d), bf), in_specs=[hbm...  42.3 us

profile of v4, /device:TPU:0, one launch (start us, length us, event | category | flops | bytes accessed | tf_op | source)
XLA Modules:
  0.0 43.0 jit_solution(16840751265515477053)
XLA Ops:
  0.0 42.3 %ffn.1 = bf16[16,4608]{1,0:T(8,128)(2,1)S(1)} custom-call(bf16[16,4608]{1,0:T(8,128)(2,1)} %stream_hbm.1, f32[4608]{0:T(1024)} %pre_hbm.1, bf16[4608,384]{1,0:T(8,128)(2,1)} %wg_hbm.1, bf16[4608,384]{1,0:T(8,128)(2,1)} %wu_hbm.1, bf16[384,4608]{1,0:T(8,128)(2,1)} %wd_hbm.1, f32[4608]{0:T(1024)} %post_hbm.1), custom_call_target="tpu_custom_call" | custom-call | tf_op jit(solution)/shard_map/ffn/pallas_call | solution.py:418
  42.3 0.7 %copy.8 = bf16[16,4608]{1,0:T(8,128)(2,1)} copy(bf16[16,4608]{1,0:T(8,128)(2,1)S(1)} %ffn.1) | data formatting | bytes 294912

commit v5 on v4

--- a/solution.py
+++ b/solution.py
@@ -10,7 +10,7 @@
 norm_eps = 1e-06
 SIDE = 2
 PLANE = SIDE * SIDE
-OUT_END, OUT_MID, BACK_END, BACK_MID = 7, 3, 4, 4
+OUT_END, OUT_MID, BACK_END, BACK_MID = 8, 3, 4, 4
 LINE = 4
 MESH = pl.DeviceIdType.MESH
 
@@ -356,49 +356,49 @@
         gath[blk(p, 0), :] = normed()
         pl.semaphore_wait(barrier, 4 + p)
         programs = ((
-                (start,), (relay_a, 0), (pass_a, 1), (spread, 2), (pass_b, 1), (zo, 1), (spread, 3), (pass_a, 2),
-                (relay_a, 1), (zc, 1, 2), (zc, 1, 1), (relay_b, 1), (spread, 1), (relay_b, 0), (pass_b, 2),
-                (zc, 1, 3), (zo, 2), (relay_a, 2), (pass_a, 3), (first, 1, 1), (zc, 2, 2), (zc, 2, 1), (relay_b, 2),
-                (last, 1, 1), (pass_b, 3), (turn, 1), (out_diag, 1), (first, 0, 1), (zc, 2, 3), (zo, 3), (relay_a, 3),
-                (last, 0, 1), (zc, 3, 1), (out_side, 0), (first, 2, 1), (zc, 3, 2), (relay_b, 3), (last, 2, 1),
-                (zc, 3, 3), (turn, 2), (out_side, 2), (pass_on_a, 1), (out_diag, 2), (out_side, 1), (pass_on_b, 1),
-                (first, 3, 1), (last, 3, 1), (out_diag, 3), (turn, 3), (pass_on_a, 2), (settle_a, 1), (pass_on_b, 2),
-                (settle_b, 1), (pass_on_a, 3), (out_side, 3), (out_diag, 0), (pass_on_b, 3), (settle_b, 2),
-                (settle_a, 2), (share,), (settle_a, 3), (pass_on_a, 0), (pass_on_b, 0), (settle_b, 3), (settle_a, 0),
-                (gain,), (settle_b, 0), (close,), (finish,), (drain,),
+                (start,), (relay_a, 0), (relay_b, 0), (pass_a, 1), (spread, 1), (spread, 2), (pass_b, 1), (zo, 1),
+                (pass_a, 2), (spread, 3), (relay_b, 1), (zc, 1, 2), (relay_a, 1), (pass_b, 2), (zc, 1, 3), (zo, 2),
+                (relay_a, 2), (pass_a, 3), (zc, 2, 1), (first, 0, 1), (zc, 1, 1), (relay_b, 2), (zc, 2, 2),
+                (pass_b, 3), (first, 1, 1), (zo, 3), (last, 1, 1), (relay_a, 3), (zc, 2, 3), (turn, 1), (out_diag, 1),
+                (last, 0, 1), (out_side, 0), (zc, 3, 1), (relay_b, 3), (first, 2, 1), (zc, 3, 2), (last, 2, 1),
+                (out_diag, 2), (turn, 2), (out_side, 2), (pass_on_a, 1), (zc, 3, 3), (pass_on_b, 1), (first, 3, 1),
+                (pass_on_b, 2), (pass_on_a, 2), (last, 3, 1), (turn, 3), (out_diag, 3), (out_side, 3), (settle_a, 2),
+                (settle_b, 2), (pass_on_b, 3), (pass_on_a, 3), (out_diag, 0), (out_side, 1), (share,), (settle_b, 3),
+                (settle_a, 3), (pass_on_a, 0), (pass_on_b, 0), (settle_a, 1), (settle_b, 1), (settle_a, 0),
+                (settle_b, 0), (gain,), (close,), (finish,), (drain,),
             ), (
-                (start,), (pass_a, 0), (relay_a, 1), (pass_a, 2), (pass_b, 0), (spread, 2), (spread, 1), (zo, 0),
-                (pass_b, 2), (spread, 3), (zo, 2), (relay_a, 0), (pass_a, 3), (zc, 2, 1), (zc, 0, 2), (zc, 2, 2),
-                (relay_a, 2), (relay_b, 0), (pass_b, 3), (zc, 0, 3), (zo, 3), (relay_b, 2), (zc, 2, 3), (relay_a, 3),
-                (zc, 3, 1), (zc, 0, 1), (first, 0, 1), (zc, 3, 2), (last, 0, 1), (zc, 3, 3), (turn, 0), (relay_b, 3),
-                (relay_b, 1), (out_diag, 0), (out_side, 0), (first, 2, 1), (last, 2, 1), (out_diag, 2), (out_side, 2),
-                (first, 3, 1), (pass_on_b, 0), (last, 3, 1), (turn, 3), (out_diag, 3), (out_side, 3), (first, 1, 1),
-                (pass_on_b, 2), (pass_on_a, 0), (last, 1, 1), (out_side, 1), (out_diag, 1), (pass_on_a, 2),
-                (pass_on_b, 3), (turn, 2), (settle_b, 0), (settle_a, 0), (pass_on_a, 3), (pass_on_b, 1),
-                (settle_a, 3), (share,), (pass_on_a, 1), (settle_b, 2), (settle_b, 3), (settle_a, 2), (settle_b, 1),
-                (settle_a, 1), (gain,), (close,), (finish,), (drain,),
+                (start,), (pass_a, 0), (relay_a, 1), (relay_b, 1), (pass_b, 0), (pass_a, 2), (spread, 1), (spread, 2),
+                (zo, 0), (pass_b, 2), (pass_a, 3), (spread, 3), (zo, 2), (relay_a, 0), (zc, 2, 1), (zc, 2, 2),
+                (zc, 0, 1), (first, 1, 1), (zc, 0, 2), (relay_b, 0), (pass_b, 3), (last, 1, 1), (zo, 3), (relay_a, 2),
+                (out_diag, 1), (relay_b, 2), (zc, 2, 3), (zc, 0, 3), (zc, 3, 1), (relay_a, 3), (zc, 3, 2),
+                (relay_b, 3), (first, 0, 1), (last, 0, 1), (zc, 3, 3), (out_diag, 0), (out_side, 0), (turn, 0),
+                (first, 2, 1), (pass_on_b, 1), (pass_on_a, 1), (last, 2, 1), (out_diag, 2), (out_side, 2),
+                (first, 3, 1), (last, 3, 1), (turn, 3), (out_diag, 3), (pass_on_b, 0), (out_side, 3), (pass_on_a, 0),
+                (pass_on_b, 2), (out_side, 1), (pass_on_a, 2), (turn, 2), (pass_on_b, 3), (pass_on_a, 3),
+                (settle_b, 0), (settle_a, 0), (settle_b, 1), (settle_a, 2), (settle_a, 3), (settle_b, 3),
+                (settle_a, 1), (settle_b, 2), (share,), (gain,), (close,), (finish,), (drain,),
             ), (
                 (start,), (pass_a, 2), (pass_a, 0), (relay_a, 1), (spread, 1), (spread, 2), (pass_b, 0), (pass_b, 2),
-                (zo, 2), (zo, 0), (pass_a, 3), (spread, 3), (pass_b, 3), (zc, 2, 2), (zc, 2, 1), (zc, 0, 1),
-                (relay_a, 0), (relay_b, 0), (zo, 3), (zc, 0, 2), (zc, 2, 3), (zc, 0, 3), (relay_b, 2), (zc, 3, 2),
-                (relay_a, 3), (zc, 3, 3), (relay_b, 3), (relay_b, 1), (first, 0, 1), (relay_a, 2), (zc, 3, 1),
-                (last, 0, 1), (out_diag, 0), (turn, 0), (out_side, 0), (first, 3, 1), (last, 3, 1), (turn, 3),
-                (out_diag, 3), (out_side, 3), (first, 1, 1), (pass_on_a, 0), (pass_on_b, 0), (last, 1, 1),
-                (out_diag, 1), (first, 2, 1), (pass_on_a, 3), (last, 2, 1), (out_diag, 2), (pass_on_b, 3),
-                (out_side, 1), (turn, 2), (settle_b, 0), (out_side, 2), (settle_a, 0), (pass_on_a, 1), (pass_on_b, 1),
-                (pass_on_a, 2), (settle_a, 3), (settle_b, 3), (share,), (pass_on_b, 2), (settle_b, 1), (settle_a, 1),
-                (settle_a, 2), (settle_b, 2), (gain,), (close,), (finish,), (drain,),
+                (zo, 0), (pass_a, 3), (zo, 2), (spread, 3), (pass_b, 3), (zc, 2, 1), (zc, 2, 2), (relay_a, 0),
+                (relay_b, 0), (zc, 0, 1), (zo, 3), (zc, 2, 3), (zc, 0, 2), (relay_b, 2), (zc, 3, 1), (relay_a, 3),
+                (zc, 0, 3), (relay_b, 3), (relay_b, 1), (zc, 3, 2), (zc, 3, 3), (first, 0, 1), (relay_a, 2),
+                (last, 0, 1), (out_side, 0), (out_diag, 0), (turn, 0), (first, 3, 1), (last, 3, 1), (out_diag, 3),
+                (out_side, 3), (turn, 3), (first, 1, 1), (first, 2, 1), (pass_on_a, 0), (pass_on_b, 0), (last, 2, 1),
+                (out_diag, 2), (pass_on_a, 3), (out_side, 2), (last, 1, 1), (pass_on_b, 3), (out_diag, 1),
+                (out_side, 1), (turn, 2), (settle_a, 0), (settle_b, 0), (pass_on_b, 2), (pass_on_a, 2), (settle_a, 3),
+                (settle_b, 3), (share,), (pass_on_b, 1), (pass_on_a, 1), (settle_a, 2), (settle_b, 2), (settle_a, 1),
+                (gain,), (settle_b, 1), (close,), (finish,), (drain,),
             ), (
                 (start,), (relay_a, 0), (pass_a, 1), (spread, 1), (spread, 2), (pass_b, 1), (zo, 1), (relay_b, 0),
-                (pass_a, 2), (spread, 3), (zc, 1, 1), (zc, 1, 2), (relay_a, 1), (pass_b, 2), (relay_b, 1), (zo, 2),
-                (first, 0, 1), (pass_a, 3), (zc, 1, 3), (relay_a, 2), (pass_b, 3), (zc, 2, 2), (relay_b, 2),
-                (zc, 2, 1), (zo, 3), (first, 1, 1), (zc, 2, 3), (relay_a, 3), (last, 1, 1), (zc, 3, 2), (relay_b, 3),
-                (turn, 1), (out_side, 1), (out_diag, 1), (zc, 3, 3), (first, 2, 1), (last, 2, 1), (zc, 3, 1),
-                (out_diag, 2), (out_side, 2), (turn, 2), (first, 3, 1), (pass_on_b, 1), (last, 3, 1), (out_diag, 3),
-                (turn, 3), (pass_on_a, 1), (pass_on_b, 2), (pass_on_a, 2), (pass_on_b, 3), (settle_b, 1),
-                (settle_a, 1), (pass_on_a, 3), (out_side, 3), (settle_a, 2), (last, 0, 1), (out_diag, 0),
-                (settle_b, 2), (out_side, 0), (settle_a, 3), (settle_b, 3), (pass_on_a, 0), (share,), (pass_on_b, 0),
-                (settle_a, 0), (gain,), (settle_b, 0), (close,), (finish,), (drain,),
+                (pass_a, 2), (zc, 1, 1), (zc, 1, 2), (spread, 3), (relay_a, 1), (pass_b, 2), (relay_b, 1),
+                (first, 0, 1), (zo, 2), (pass_a, 3), (pass_b, 3), (relay_a, 2), (zc, 1, 3), (zc, 2, 1), (zc, 2, 2),
+                (relay_b, 2), (zo, 3), (first, 1, 1), (zc, 2, 3), (relay_b, 3), (relay_a, 3), (last, 1, 1),
+                (out_side, 1), (zc, 3, 1), (turn, 1), (out_diag, 1), (first, 2, 1), (zc, 3, 2), (last, 2, 1),
+                (out_diag, 2), (turn, 2), (out_side, 2), (zc, 3, 3), (first, 3, 1), (last, 3, 1), (pass_on_b, 1),
+                (out_diag, 3), (turn, 3), (pass_on_a, 1), (pass_on_a, 2), (pass_on_b, 2), (settle_b, 1),
+                (pass_on_b, 3), (pass_on_a, 3), (out_side, 3), (settle_a, 1), (settle_a, 2), (settle_b, 2),
+                (last, 0, 1), (out_diag, 0), (out_side, 0), (settle_a, 3), (settle_b, 3), (pass_on_a, 0),
+                (pass_on_b, 0), (share,), (settle_a, 0), (settle_b, 0), (gain,), (close,), (finish,), (drain,),
             ))
         for f, *args in programs[v]:
             with jax.named_scope("#".join([f.__name__, *map(str, args)])):

time: 43.4 us -> 43 us (level)
  no operation moved by 1% of the time
where the time goes in v5:
time: 43 us; the launch traced here: 42.9 us
  Pallas kernels  42.2 us (98%)
  local copies, waits for them, and re-layouts  0.66 us (2%)
    pallas_call x1, Pallas kernels, fused(): pl.pallas_call(kernel, out_shape=pltpu.VMEM((rows, d), bf), in_specs=[hbm...  42.2 us

profile of v5, /device:TPU:0, one launch (start us, length us, event | category | flops | bytes accessed | tf_op | source)
XLA Modules:
  0.0 42.9 jit_solution(18254948909635626056)
XLA Ops:
  0.0 42.2 %ffn.1 = bf16[16,4608]{1,0:T(8,128)(2,1)S(1)} custom-call(bf16[16,4608]{1,0:T(8,128)(2,1)} %stream_hbm.1, f32[4608]{0:T(1024)} %pre_hbm.1, bf16[4608,384]{1,0:T(8,128)(2,1)} %wg_hbm.1, bf16[4608,384]{1,0:T(8,128)(2,1)} %wu_hbm.1, bf16[384,4608]{1,0:T(8,128)(2,1)} %wd_hbm.1, f32[4608]{0:T(1024)} %post_hbm.1), custom_call_target="tpu_custom_call" | custom-call | tf_op jit(solution)/shard_map/ffn/pallas_call | solution.py:418
  42.2 0.7 %copy.8 = bf16[16,4608]{1,0:T(8,128)(2,1)} copy(bf16[16,4608]{1,0:T(8,128)(2,1)S(1)} %ffn.1) | data formatting | bytes 294912
